TPU v7x, 32 devices: a whole 2x2x4 slice. The times are simulated.
32 devices in a mesh: blk: 8 (over z, y), rep: 4 (over x, core).
Axes of the slice: x: 2, y: 2, z: 4, core: 2. Of those that a mesh axis runs over, the one named last changes fastest.
Arguments:
- embeddings: bfloat16 [3072, 1024], P(('blk', 'rep')), may hold values from -60 to 60, as said below
Outputs:
- nearest: float32 [3072, 8], P(('blk', 'rep'))
- dup_count: float32 [3072], P(('blk', 'rep'))
Inputs may be any that keep to these rules, and one draw needn't show every extreme that they name: Real-valued embeddings; no row is zero.
All inputs are finite; a program needn't handle non-finite values.
Results may differ from a plain program's by a relative error of at most 0.00068.
Values may be sent and summed in bfloat16 or wider, within the bound.
No kernel may reach another device: no remote copies, remote signals or barrier semaphores. Data moves between devices by JAX's collectives and lax.ppermute only.
A program may use at most 128 MiB of HBM per device.

v0:
```python
import functools
import math

import jax
import jax.numpy as jnp
from jax import lax
from jax.experimental import pallas as pl
from jax.experimental.pallas import tpu as pltpu
from jax.sharding import PartitionSpec as P


TOPK = 8
SUB = 8
PACK = 16
LOW = -4.0
decision_bound = 0.5
sigmoid_sharpness = 0.05
GRANT = 32 * 2**20
AXES = ("blk", "rep")

SOFT_SLOPE = 1.0 / (sigmoid_sharpness * math.log(2.0))
SOFT_BASE = decision_bound * SOFT_SLOPE


SORT8 = (
    (0, 1), (2, 3), (4, 5), (6, 7),
    (0, 2), (1, 3), (4, 6), (5, 7),
    (1, 2), (5, 6), (0, 4), (3, 7),
    (1, 5), (2, 6),
    (1, 4), (3, 6),
    (2, 4), (3, 5),
    (3, 4),
)
BITONIC8 = (
    (0, 4), (1, 5), (2, 6), (3, 7),
    (0, 2), (1, 3), (4, 6), (5, 7),
    (0, 1), (2, 3), (4, 5), (6, 7),
)


def network(values, pairs):
    values = list(values)
    for low, high in pairs:
        a, b = values[low], values[high]
        values[low], values[high] = jnp.maximum(a, b), jnp.minimum(a, b)
    return values


def merge(a, b):
    return network([jnp.maximum(a[i], b[TOPK - 1 - i]) for i in range(TOPK)], BITONIC8)


def soft(table):
    return 1.0 / (1.0 + jnp.exp2(SOFT_BASE - SOFT_SLOPE * table))


def column_lists(table):
    tiles = [table[i : i + SUB] for i in range(0, table.shape[0], SUB)]
    best = None
    for i in range(0, len(tiles), TOPK):
        group = tiles[i : i + TOPK]
        group += [jnp.full_like(tiles[0], LOW)] * (TOPK - len(group))
        group = network(group, SORT8)
        best = group if best is None else merge(best, group)
    count = functools.reduce(jnp.add, [soft(t) for t in tiles])
    return best, count


def fold_sublanes(best, count):
    for step in (4, 2, 1):
        best = merge(best, [pltpu.roll(b, step, 0) for b in best])
        count = count + pltpu.roll(count, step, 0)
    place = lax.broadcasted_iota(jnp.int32, best[0].shape, 0)
    top = best[0]
    for i in range(1, TOPK):
        top = jnp.where(place == i, best[i], top)
    return top, count


def dots(a, b):
    return lax.dot_general(a, b, (((1,), (1,)), ((), ())), preferred_element_type=jnp.float32)


def unit_rows(block):
    whole = block.astype(jnp.float32)
    length = jnp.sqrt(jnp.sum(whole * whole, axis=1, keepdims=True) + 1e-06)
    return (whole / length).astype(jnp.bfloat16)


def unit_kernel(x_ref, o_ref):
    o_ref[...] = unit_rows(x_ref[...])


def join_kernel(a_ref, b_ref, o_ref):
    rows = a_ref.shape[0]
    o_ref[:rows] = a_ref[...]
    o_ref[rows:] = b_ref[...]


def store(ref, top, total, start=0):
    columns = pl.ds(start, top.shape[1])
    ref[:SUB, columns] = top
    ref[SUB:, columns] = total


def split_queries(pair, direct, relayed, corner, corner_twin):
    rows = corner.shape[0]
    keep = jnp.concatenate([pair[:rows], direct[...], corner[...]], axis=0)
    give = jnp.concatenate([pair[rows:], relayed[...], corner_twin[...]], axis=0)
    return keep, give


def home_kernel(diagonal, pair, *refs):
    *others, ref = refs
    rows = pair.shape[0] // 2
    first = pair[:rows] if diagonal else pair[rows:]
    table = dots(pair[:rows], jnp.concatenate([first] + [o[...] for o in others], axis=0))
    if diagonal:
        line = lax.broadcasted_iota(jnp.int32, table.shape, 0)
        column = lax.broadcasted_iota(jnp.int32, table.shape, 1)
        table = jnp.where(line == column, -2.0, table)
    best, count = column_lists(table)
    for i in range(TOPK):
        ref[i * SUB : (i + 1) * SUB] = best[i]
    ref[TOPK * SUB :] = count


def score_kernel(n_shift, got, *refs):
    queries, states = refs[:5], refs[5:7]
    pairs = refs[7 : 7 + 2 * n_shift]
    keep_ref, give_ref = refs[7 + 2 * n_shift : 9 + 2 * n_shift]
    back_refs = refs[9 + 2 * n_shift :]
    first = lax.axis_index("rep") % 2 == 0
    key = [jnp.where(first, a[...], b[...]) for a, b in zip(pairs[::2], pairs[1::2])]
    live = got()
    keep, give = split_queries(*queries)
    down = [(dots(keep, k), dots(give, k)) for k in key]
    ahead = [d[0].T for d in down]
    for k in range(n_shift):
        table = jnp.concatenate(down[k], axis=0)
        store(back_refs[k], *fold_sublanes(*column_lists(table)))
    for query, state, ref in ((keep, states[0], keep_ref), (give, states[1], give_ref)):
        best = [state[i * SUB : (i + 1) * SUB] for i in range(TOPK)]
        count = state[TOPK * SUB :]
        tables, ahead = ahead, [d[1].T for d in down] if query is keep else None
        for k in range(n_shift):
            more, more_count = column_lists(tables[k])
            best = merge(best, [jnp.where(live[k], m, LOW) for m in more])
            count = count + jnp.where(live[k], more_count, 0.0)
        store(ref, *fold_sublanes(best, count))


def lists_of(packed):
    shape = (SUB, packed.shape[1])
    row = lambda i: jnp.broadcast_to(packed[i : i + 1], shape)
    return [row(i) for i in range(TOPK)], packed[SUB:]


def stacked(best):
    place = lax.broadcasted_iota(jnp.int32, best[0].shape, 0)
    top = best[0]
    for i in range(1, TOPK):
        top = jnp.where(place == i, best[i], top)
    return top


def pair_kernel(keep_ref, got_ref, own_ref, direct_ref, corner_ref):
    rows = own_ref.shape[1]
    best, count = lists_of(keep_ref[...])
    more, more_count = lists_of(got_ref[...])
    top, total = stacked(merge(best, more)), count + more_count
    store(own_ref, top[:, :rows], total[:, :rows])
    store(direct_ref, top[:, rows : 3 * rows], total[:, rows : 3 * rows])
    store(corner_ref, top[:, 3 * rows :], total[:, 3 * rows :])


def last_kernel(n_shift, gave, own, corner, direct, relayed, *refs):
    mine, theirs = refs[:n_shift], refs[n_shift : 2 * n_shift]
    near_ref, dup_ref = refs[2 * n_shift :]
    rows = own.shape[1]
    found = [lists_of(own[...]), lists_of(corner[...])]
    found += [lists_of(direct[:, :rows]), lists_of(relayed[:, rows:])]
    parts = [m[:, :rows] for m in mine] + [t[:, rows:] for t in theirs]
    for flag, part in zip(gave(False) + gave(True), parts):
        best, count = lists_of(part)
        found.append(([jnp.where(flag, b, LOW) for b in best], jnp.where(flag, count, 0.0)))
    while len(found) > 1:
        paired = [
            (merge(found[i][0], found[i + 1][0]), found[i][1] + found[i + 1][1])
            for i in range(0, len(found) - 1, 2)
        ]
        found = paired + found[len(found) - len(found) % 2 :]
    best, count = found[0]
    near_ref[...] = stacked(best)
    dup_ref[...] = count[:1]


VMEM = pl.BlockSpec(memory_space=pltpu.VMEM)


def call(kernel, args, shapes, keep=True):
    args = [pltpu.with_memory_space_constraint(a, pltpu.VMEM) for a in args]
    return pl.pallas_call(
        kernel,
        out_shape=[(pltpu.VMEM if keep else jax.ShapeDtypeStruct)(*s) for s in shapes],
        in_specs=[VMEM] * len(args),
        out_specs=[VMEM] * len(shapes),
        compiler_params=pltpu.CompilerParams(vmem_limit_bytes=GRANT),
    )(*args)


def body(blocks, reps, embeddings):
    rows, width = embeddings.shape
    deep, wide = blocks // 2, reps // 2
    half = deep // 2
    n_shift = (half + 1) // 2
    f32, bf16 = jnp.float32, jnp.bfloat16

    def flat(z, y, x, c):
        return ((z * 2 + y) * wide + x) * 2 + c

    places = [
        (z, y, x, c) for z in range(deep) for y in range(2) for x in range(wide) for c in range(2)
    ]

    def moved(value, to, reverse=False, cores=(0, 1)):
        perm = [
            (flat(*p), flat(*to(*p))) for p in places if p[3] in cores and to(*p) is not None
        ]
        return lax.ppermute(value, AXES, [(b, a) for a, b in perm] if reverse else perm)

    def swap(z, y, x, c):
        return z, y, x, 1 - c

    def side(z, y, x, c):
        return (z, y, (x + 1) % wide, c) if c == 0 else (z, 1 - y, x, c)

    def corner(z, y, x, c):
        return z, 1 - y, (x + 1) % wide, c

    def shift(j):
        def to(z, y, x, c):
            k = 2 * j + 2 - c
            if k > half:
                return None
            if 2 * k == deep:
                if z < half:
                    return (z + half, y, x, c) if z % 2 == 0 else None
                return (z - half, y, x, c) if (z - half) % 2 == 1 else None
            return (z + k) % deep, y, x, c

        return to

    def flags(other, pick):
        depth = lax.axis_index("blk") // 2
        core = lax.axis_index("rep") % 2
        core = 1 - core if other else core
        sends = jnp.where(depth < half, depth % 2 == 0, (depth - half) % 2 == 1)
        out = []
        for j in range(n_shift):
            k = 2 * j + 2 - core
            whole = 2 * k != deep
            out.append((k <= half) & (whole | (sends == pick)))
        return out

    def gave(other):
        return flags(other, True)

    def got():
        return flags(False, False)

    (unit,) = call(unit_kernel, [embeddings], [((rows, width), bf16)])
    twin = moved(unit, swap)
    corner_rows = moved(unit, corner)
    (pair,) = call(join_kernel, [unit, twin], [((2 * rows, width), bf16)])
    keys = []
    for j in range(n_shift):
        keys += [moved(pair, shift(j), cores=(c,)) for c in range(2)]
    direct = moved(pair, side)
    corner_twin = moved(corner_rows, swap)
    relayed = moved(direct, swap)
    queries = [pair, direct, relayed, corner_rows, corner_twin]

    state = (((TOPK + 1) * SUB, 4 * rows), f32)
    states = call(functools.partial(home_kernel, True), [pair, direct, corner_rows], [state])
    states += call(functools.partial(home_kernel, False), [pair, relayed, corner_twin], [state])
    lists = lambda n: ((PACK, n * rows), f32)
    keep, give, *away = call(
        functools.partial(score_kernel, n_shift, got),
        queries + list(states) + keys,
        [lists(4), lists(4)] + [lists(2)] * n_shift,
    )
    given = moved(give, swap)
    mine = [moved(a, shift(j), reverse=True) for j, a in enumerate(away)]
    own, sides, corners = call(pair_kernel, [keep, given], [lists(1), lists(2), lists(1)])
    direct = moved(sides, side, reverse=True)
    corners = moved(corners, corner, reverse=True)
    theirs = [moved(m, swap) for m in mine]
    relayed = moved(direct, swap)
    near, dup = call(
        functools.partial(last_kernel, n_shift, gave),
        [own, corners, direct, relayed] + mine + theirs,
        [((TOPK, rows), f32), ((1, rows), f32)],
        keep=False,
    )
    return near.T, dup.reshape(rows)


def solution(mesh):
    placed = (P(AXES, None),)

    def layer(embeddings):
        return body(mesh.shape["blk"], mesh.shape["rep"], embeddings)

    return jax.shard_map(
        layer,
        mesh=mesh,
        in_specs=placed,
        out_specs=(P(AXES, None), P(AXES)),
        check_vma=False,
    )
```

profile of v0, /device:TPU:0, one launch (start us, length us, event | category | flops | bytes accessed | tf_op | source)
XLA Modules:
  0.0 42.4 jit_solution(12992694342362752916)
XLA Ops:
  0.6 0.9 %copy-done = bf16[96,1024]{1,0:T(8,128)(2,1)S(1)} copy-done((bf16[96,1024]{1,0:T(8,128)(2,1)S(1)}, bf16[96,1024]{1,0:T(8,128)(2,1)}, u32[]{:S(2)}) %copy-start) | copy-done | bytes 196632
  1.6 0.1 shard_map.30.a_ref
  1.7 0.6 %collective-permute-start = (bf16[96,1024]{1,0:T(8,128)(2,1)S(1)}, bf16[96,1024]{1,0:T(8,128)(2,1)S(1)}, u32[]{:S(2)}, u32[]{:S(2)}) collective-permute-start(bf16[96,1024]{1,0:T(8,128)(2,1)S(1)} %shard_map.30.a_ref), channel_id=1, source_target_pairs={{0,1},{1,0},{2,3},{3,2},{4,5},{5,4},{6,7},{7,6},{8,9},{9,8},{10,11... | collective-permute-start | bytes 589832 | tf_op jit(solution)/shard_map/ppermute | solution.py:230
  2.3 1.1 %collective-permute-done.b_ref = bf16[96,1024]{1,0:T(8,128)(2,1)S(1)} collective-permute-done((bf16[96,1024]{1,0:T(8,128)(2,1)S(1)}, bf16[96,1024]{1,0:T(8,128)(2,1)S(1)}, u32[]{:S(2)}, u32[]{:S(2)}) %collective-permute-start) | collective-permute-done | bytes 196640 | tf_op jit(solution)/shard_map/ppermute | solution.py:230
  3.4 2.9 %collective-permute-start.1 = (bf16[192,1024]{1,0:T(8,128)(2,1)S(1)}, bf16[192,1024]{1,0:T(8,128)(2,1)S(1)}, u32[]{:S(2)}, u32[]{:S(2)}) collective-permute-start(bf16[192,1024]{1,0:T(8,128)(2,1)S(1)} %shard_map.31.pair.refs_0_), channel_id=1, source_target_pairs={{0,2},{1,5},{2,0},{3,7},{4,6},{5,1},{6,4},{7,3},{8,10},{9,13},{10,... | collective-permute-start | bytes 1179656 | tf_op jit(solution)/shard_map/ppermute | solution.py:230
  6.3 1.5 %collective-permute-start.3 = (bf16[96,1024]{1,0:T(8,128)(2,1)S(1)}, bf16[96,1024]{1,0:T(8,128)(2,1)S(1)}, u32[]{:S(2)}, u32[]{:S(2)}) collective-permute-start(bf16[96,1024]{1,0:T(8,128)(2,1)S(1)} %shard_map.30.a_ref), channel_id=1, source_target_pairs={{0,6},{1,7},{2,4},{3,5},{4,2},{5,3},{6,0},{7,1},{8,14},{9,15},{10,... | collective-permute-start | bytes 589832 | tf_op jit(solution)/shard_map/ppermute | solution.py:230
  7.8 6.4 %collective-permute-done.1.refs_0_.refs_1_ = bf16[192,1024]{1,0:T(8,128)(2,1)S(1)} collective-permute-done((bf16[192,1024]{1,0:T(8,128)(2,1)S(1)}, bf16[192,1024]{1,0:T(8,128)(2,1)S(1)}, u32[]{:S(2)}, u32[]{:S(2)}) %collective-permute-start.1) | collective-permute-done | bytes 393248 | tf_op jit(solution)/shard_map/ppermute | solution.py:230
  14.1 0.0 collective-permute-start.2
  14.1 0.7 %collective-permute-start.6 = (bf16[192,1024]{1,0:T(8,128)(2,1)S(1)}, bf16[192,1024]{1,0:T(8,128)(2,1)S(1)}, u32[]{:S(2)}, u32[]{:S(2)}) collective-permute-start(bf16[192,1024]{1,0:T(8,128)(2,1)S(1)} %shard_map.31.pair.refs_0_), channel_id=1, source_target_pairs={{1,9},{3,11},{5,13},{7,15},{9,17},{11,19},{13,21},{15,23},{17,25},... | collective-permute-start | bytes 1179656 | tf_op jit(solution)/shard_map/ppermute | solution.py:230
  14.8 5.0 %collective-permute-start.5 = (bf16[192,1024]{1,0:T(8,128)(2,1)S(1)}, bf16[192,1024]{1,0:T(8,128)(2,1)S(1)}, u32[]{:S(2)}, u32[]{:S(2)}) collective-permute-start(bf16[192,1024]{1,0:T(8,128)(2,1)S(1)} %shard_map.31.pair.refs_0_), channel_id=1, source_target_pairs={{0,16},{2,18},{4,20},{6,22},{24,8},{26,10},{28,12},{30,14}} | collective-permute-start | bytes 1179656 | tf_op jit(solution)/shard_map/ppermute | solution.py:230
  19.9 0.0 collective-permute-done.3.refs_1_.refs_3_
  19.9 0.1 collective-permute-start.4
  20.0 0.4 shard_map.32.refs_5_
  20.4 1.0 %collective-permute-done.4.refs_1_.refs_4_ = bf16[96,1024]{1,0:T(8,128)(2,1)S(1)} collective-permute-done((bf16[96,1024]{1,0:T(8,128)(2,1)S(1)}, bf16[96,1024]{1,0:T(8,128)(2,1)S(1)}, u32[]{:S(2)}, u32[]{:S(2)}) %collective-permute-start.4) | collective-permute-done | bytes 196640 | tf_op jit(solution)/shard_map/ppermute | solution.py:230
  21.4 0.0 collective-permute-done.2.refs_0_.refs_2_
  21.4 0.4 shard_map.33.refs_6_
  21.8 0.0 collective-permute-done.6.refs_8_
  21.8 5.4 %collective-permute-done.5.refs_7_ = bf16[192,1024]{1,0:T(8,128)(2,1)S(1)} collective-permute-done((bf16[192,1024]{1,0:T(8,128)(2,1)S(1)}, bf16[192,1024]{1,0:T(8,128)(2,1)S(1)}, u32[]{:S(2)}, u32[]{:S(2)}) %collective-permute-start.5) | collective-permute-done | bytes 393248 | tf_op jit(solution)/shard_map/ppermute | solution.py:230
  27.2 1.3 %shard_map.34 = (f32[16,384]{1,0:T(8,128)S(1)}, f32[16,384]{1,0:T(8,128)S(1)}, f32[16,192]{1,0:T(8,128)S(1)}) custom-call(bf16[192,1024]{1,0:T(8,128)(2,1)S(1)} %shard_map.31.pair.refs_0_, bf16[192,1024]{1,0:T(8,128)(2,1)S(1)} %collective-permute-done.1.refs_0_.refs_1_, bf16[192,1024]{1,0:T(8,128)(2,1)S(1)} %collective-permute-done.2.refs_0_.refs_2_, ...), custom_call_target="tpu_custom_call" | custom-call | tf_op jit(solution)/shard_map/pallas_call | solution.py:203
  28.5 1.4 %collective-permute-start.7 = (f32[16,384]{1,0:T(8,128)S(1)}, f32[16,384]{1,0:T(8,128)S(1)}, u32[]{:S(2)}, u32[]{:S(2)}) collective-permute-start(f32[16,384]{1,0:T(8,128)S(1)} %get-tuple-element.11), channel_id=1, source_target_pairs={{0,1},{1,0},{2,3},{3,2},{4,5},{5,4},{6,7},{7,6},{8,9},{9,8},{10,11... | collective-permute-start | bytes 73736 | tf_op jit(solution)/shard_map/ppermute | solution.py:230
  30.0 1.3 %collective-permute-start.11 = (f32[16,192]{1,0:T(8,128)S(1)}, f32[16,192]{1,0:T(8,128)S(1)}, u32[]{:S(2)}, u32[]{:S(2)}) collective-permute-start(f32[16,192]{1,0:T(8,128)S(1)} %get-tuple-element.15), channel_id=1, source_target_pairs={{16,0},{9,1},{18,2},{11,3},{20,4},{13,5},{22,6},{15,7},{17,9},{19,... | collective-permute-start | bytes 36872 | tf_op jit(solution)/shard_map/ppermute | solution.py:230
  31.2 0.0 collective-permute-done.7.got_ref
  31.3 0.1 shard_map.35
  31.3 1.5 %collective-permute-start.9 = (f32[16,192]{1,0:T(8,128)S(1)}, f32[16,192]{1,0:T(8,128)S(1)}, u32[]{:S(2)}, u32[]{:S(2)}) collective-permute-start(f32[16,192]{1,0:T(8,128)S(1)} %get-tuple-element.14), channel_id=1, source_target_pairs={{2,0},{5,1},{0,2},{7,3},{6,4},{1,5},{4,6},{3,7},{10,8},{13,9},{8,1... | collective-permute-start | bytes 36872 | tf_op jit(solution)/shard_map/ppermute | solution.py:230
  32.9 3.8 %collective-permute-done.11.refs_0_ = f32[16,192]{1,0:T(8,128)S(1)} collective-permute-done((f32[16,192]{1,0:T(8,128)S(1)}, f32[16,192]{1,0:T(8,128)S(1)}, u32[]{:S(2)}, u32[]{:S(2)}) %collective-permute-start.11) | collective-permute-done | bytes 12320 | tf_op jit(solution)/shard_map/ppermute | solution.py:230
  36.6 0.0 collective-permute-start.12
  36.6 0.0 collective-permute-done.9.direct
  36.6 0.5 %collective-permute-start.10 = (f32[16,192]{1,0:T(8,128)S(1)}, f32[16,192]{1,0:T(8,128)S(1)}, u32[]{:S(2)}, u32[]{:S(2)}) collective-permute-start(f32[16,192]{1,0:T(8,128)S(1)} %collective-permute-done.9.direct), channel_id=1, source_target_pairs={{0,1},{1,0},{2,3},{3,2},{4,5},{5,4},{6,7},{7,6},{8,9},{9,8},{10,11... | collective-permute-start | bytes 36872 | tf_op jit(solution)/shard_map/ppermute | solution.py:230
  37.1 2.4 %collective-permute-start.8 = (f32[16,96]{1,0:T(8,128)S(1)}, f32[16,96]{1,0:T(8,128)S(1)}, u32[]{:S(2)}, u32[]{:S(2)}) collective-permute-start(f32[16,96]{1,0:T(8,128)S(1)} %get-tuple-element.13), channel_id=1, source_target_pairs={{6,0},{7,1},{4,2},{5,3},{2,4},{3,5},{0,6},{1,7},{14,8},{15,9},{12,... | collective-permute-start | bytes 18440 | tf_op jit(solution)/shard_map/ppermute | solution.py:230
  39.6 0.0 collective-permute-done.12.refs_1_
  39.6 2.1 %collective-permute-done.8.corner = f32[16,96]{1,0:T(8,128)S(1)} collective-permute-done((f32[16,96]{1,0:T(8,128)S(1)}, f32[16,96]{1,0:T(8,128)S(1)}, u32[]{:S(2)}, u32[]{:S(2)}) %collective-permute-start.8) | collective-permute-done | bytes 6176 | tf_op jit(solution)/shard_map/ppermute | solution.py:230
  41.7 0.7 %shard_map.36 = (f32[8,96]{1,0:T(8,128)}, f32[1,96]{1,0:T(1,128)}) custom-call(f32[16,96]{1,0:T(8,128)S(1)} %get-tuple-element.12.own, f32[16,96]{1,0:T(8,128)S(1)} %collective-permute-done.8.corner, f32[16,192]{1,0:T(8,128)S(1)} %collective-permute-done.9.direct, f32[16,192]{1,0:T(8,128)S(1)} %collective-permute-done.10.relayed, ...), custom_call_target="tpu_custom_call" | custom-call | tf_op jit(solution)/shard_map/pallas_call | solution.py:203
  (3 shorter events, 0.0 us)
Async XLA Ops:
  0.6 0.9 %copy-start = (bf16[96,1024]{1,0:T(8,128)(2,1)S(1)}, bf16[96,1024]{1,0:T(8,128)(2,1)}, u32[]{:S(2)}) copy-start(bf16[96,1024]{1,0:T(8,128)(2,1)} %x_ref.1) | copy-start | bytes 589828
  1.7 1.6 %collective-permute-start = (bf16[96,1024]{1,0:T(8,128)(2,1)S(1)}, bf16[96,1024]{1,0:T(8,128)(2,1)S(1)}, u32[]{:S(2)}, u32[]{:S(2)}) collective-permute-start(bf16[96,1024]{1,0:T(8,128)(2,1)S(1)} %shard_map.30.a_ref), channel_id=1, source_target_pairs={{0,1},{1,0},{2,3},{3,2},{4,5},{5,4},{6,7},{7,6},{8,9},{9,8},{10,11... | collective-permute-start | bytes 589832 | tf_op jit(solution)/shard_map/ppermute | solution.py:230
  3.4 10.8 %collective-permute-start.1 = (bf16[192,1024]{1,0:T(8,128)(2,1)S(1)}, bf16[192,1024]{1,0:T(8,128)(2,1)S(1)}, u32[]{:S(2)}, u32[]{:S(2)}) collective-permute-start(bf16[192,1024]{1,0:T(8,128)(2,1)S(1)} %shard_map.31.pair.refs_0_), channel_id=1, source_target_pairs={{0,2},{1,5},{2,0},{3,7},{4,6},{5,1},{6,4},{7,3},{8,10},{9,13},{10,... | collective-permute-start | bytes 1179656 | tf_op jit(solution)/shard_map/ppermute | solution.py:230
  6.3 13.6 %collective-permute-start.3 = (bf16[96,1024]{1,0:T(8,128)(2,1)S(1)}, bf16[96,1024]{1,0:T(8,128)(2,1)S(1)}, u32[]{:S(2)}, u32[]{:S(2)}) collective-permute-start(bf16[96,1024]{1,0:T(8,128)(2,1)S(1)} %shard_map.30.a_ref), channel_id=1, source_target_pairs={{0,6},{1,7},{2,4},{3,5},{4,2},{5,3},{6,0},{7,1},{8,14},{9,15},{10,... | collective-permute-start | bytes 589832 | tf_op jit(solution)/shard_map/ppermute | solution.py:230
  14.1 7.3 %collective-permute-start.2 = (bf16[192,1024]{1,0:T(8,128)(2,1)S(1)}, bf16[192,1024]{1,0:T(8,128)(2,1)S(1)}, u32[]{:S(2)}, u32[]{:S(2)}) collective-permute-start(bf16[192,1024]{1,0:T(8,128)(2,1)S(1)} %collective-permute-done.1.refs_0_.refs_1_), channel_id=1, source_target_pairs={{0,1},{1,0},{2,3},{3,2},{4,5},{5,4},{6,7},{7,6},{8,9},{9,8},{10,11... | collective-permute-start | bytes 1179656 | tf_op jit(solution)/shard_map/ppermute | solution.py:230
  14.1 7.7 %collective-permute-start.6 = (bf16[192,1024]{1,0:T(8,128)(2,1)S(1)}, bf16[192,1024]{1,0:T(8,128)(2,1)S(1)}, u32[]{:S(2)}, u32[]{:S(2)}) collective-permute-start(bf16[192,1024]{1,0:T(8,128)(2,1)S(1)} %shard_map.31.pair.refs_0_), channel_id=1, source_target_pairs={{1,9},{3,11},{5,13},{7,15},{9,17},{11,19},{13,21},{15,23},{17,25},... | collective-permute-start | bytes 1179656 | tf_op jit(solution)/shard_map/ppermute | solution.py:230
  14.8 12.4 %collective-permute-start.5 = (bf16[192,1024]{1,0:T(8,128)(2,1)S(1)}, bf16[192,1024]{1,0:T(8,128)(2,1)S(1)}, u32[]{:S(2)}, u32[]{:S(2)}) collective-permute-start(bf16[192,1024]{1,0:T(8,128)(2,1)S(1)} %shard_map.31.pair.refs_0_), channel_id=1, source_target_pairs={{0,16},{2,18},{4,20},{6,22},{24,8},{26,10},{28,12},{30,14}} | collective-permute-start | bytes 1179656 | tf_op jit(solution)/shard_map/ppermute | solution.py:230
  19.9 1.5 %collective-permute-start.4 = (bf16[96,1024]{1,0:T(8,128)(2,1)S(1)}, bf16[96,1024]{1,0:T(8,128)(2,1)S(1)}, u32[]{:S(2)}, u32[]{:S(2)}) collective-permute-start(bf16[96,1024]{1,0:T(8,128)(2,1)S(1)} %collective-permute-done.3.refs_1_.refs_3_), channel_id=1, source_target_pairs={{0,1},{1,0},{2,3},{3,2},{4,5},{5,4},{6,7},{7,6},{8,9},{9,8},{10,11... | collective-permute-start | bytes 589832 | tf_op jit(solution)/shard_map/ppermute | solution.py:230
  28.5 2.7 %collective-permute-start.7 = (f32[16,384]{1,0:T(8,128)S(1)}, f32[16,384]{1,0:T(8,128)S(1)}, u32[]{:S(2)}, u32[]{:S(2)}) collective-permute-start(f32[16,384]{1,0:T(8,128)S(1)} %get-tuple-element.11), channel_id=1, source_target_pairs={{0,1},{1,0},{2,3},{3,2},{4,5},{5,4},{6,7},{7,6},{8,9},{9,8},{10,11... | collective-permute-start | bytes 73736 | tf_op jit(solution)/shard_map/ppermute | solution.py:230
  30.0 6.7 %collective-permute-start.11 = (f32[16,192]{1,0:T(8,128)S(1)}, f32[16,192]{1,0:T(8,128)S(1)}, u32[]{:S(2)}, u32[]{:S(2)}) collective-permute-start(f32[16,192]{1,0:T(8,128)S(1)} %get-tuple-element.15), channel_id=1, source_target_pairs={{16,0},{9,1},{18,2},{11,3},{20,4},{13,5},{22,6},{15,7},{17,9},{19,... | collective-permute-start | bytes 36872 | tf_op jit(solution)/shard_map/ppermute | solution.py:230
  31.3 5.3 %collective-permute-start.9 = (f32[16,192]{1,0:T(8,128)S(1)}, f32[16,192]{1,0:T(8,128)S(1)}, u32[]{:S(2)}, u32[]{:S(2)}) collective-permute-start(f32[16,192]{1,0:T(8,128)S(1)} %get-tuple-element.14), channel_id=1, source_target_pairs={{2,0},{5,1},{0,2},{7,3},{6,4},{1,5},{4,6},{3,7},{10,8},{13,9},{8,1... | collective-permute-start | bytes 36872 | tf_op jit(solution)/shard_map/ppermute | solution.py:230
  36.6 3.0 %collective-permute-start.12 = (f32[16,192]{1,0:T(8,128)S(1)}, f32[16,192]{1,0:T(8,128)S(1)}, u32[]{:S(2)}, u32[]{:S(2)}) collective-permute-start(f32[16,192]{1,0:T(8,128)S(1)} %collective-permute-done.11.refs_0_), channel_id=1, source_target_pairs={{0,1},{1,0},{2,3},{3,2},{4,5},{5,4},{6,7},{7,6},{8,9},{9,8},{10,11... | collective-permute-start | bytes 36872 | tf_op jit(solution)/shard_map/ppermute | solution.py:230
  36.6 5.1 %collective-permute-start.10 = (f32[16,192]{1,0:T(8,128)S(1)}, f32[16,192]{1,0:T(8,128)S(1)}, u32[]{:S(2)}, u32[]{:S(2)}) collective-permute-start(f32[16,192]{1,0:T(8,128)S(1)} %collective-permute-done.9.direct), channel_id=1, source_target_pairs={{0,1},{1,0},{2,3},{3,2},{4,5},{5,4},{6,7},{7,6},{8,9},{9,8},{10,11... | collective-permute-start | bytes 36872 | tf_op jit(solution)/shard_map/ppermute | solution.py:230
  37.1 4.5 %collective-permute-start.8 = (f32[16,96]{1,0:T(8,128)S(1)}, f32[16,96]{1,0:T(8,128)S(1)}, u32[]{:S(2)}, u32[]{:S(2)}) collective-permute-start(f32[16,96]{1,0:T(8,128)S(1)} %get-tuple-element.13), channel_id=1, source_target_pairs={{6,0},{7,1},{4,2},{5,3},{2,4},{3,5},{0,6},{1,7},{14,8},{15,9},{12,... | collective-permute-start | bytes 18440 | tf_op jit(solution)/shard_map/ppermute | solution.py:230
where the time goes:
time: 42.6 us; the launch traced here: 42.4 us
  waiting for transfers between devices  19.7 us (46%)
  starting transfers between devices  17.9 us (42%)
  Pallas kernels  3.13 us (7%)
  local copies, waits for them, and re-layouts  0.92 us (2%)
  between operations  0.73 us (2%)
    ppermute x13, waiting for transfers between devices, moved(): lax.ppermute(value, AXES, [(b, a) for a, b in perm] if reverse else perm)  19.7 us
    ppermute x13, starting transfers between devices, moved(): lax.ppermute(value, AXES, [(b, a) for a, b in perm] if reverse else perm)  17.9 us
    pallas_call x7, Pallas kernels, call(): pl.pallas_call(kernel, out_shape=[(pltpu.VMEM if keep else jax.ShapeDtype...  3.13 us
    unnamed x2, local copies, waits for them, and re-layouts  0.92 us
  transfers between devices with their start and end apart: 13, of which 6 were waited for; matrix products, arithmetic and copies ran while one was open for 0% of the time, Pallas kernels for 2%

commit v1 on v0

--- a/solution.py
+++ b/solution.py
@@ -127,13 +127,12 @@
 
 def score_kernel(n_shift, got, *refs):
     queries, states = refs[:5], refs[5:7]
-    pairs = refs[7 : 7 + 2 * n_shift]
-    keep_ref, give_ref = refs[7 + 2 * n_shift : 9 + 2 * n_shift]
-    back_refs = refs[9 + 2 * n_shift :]
-    first = lax.axis_index("rep") % 2 == 0
-    key = [jnp.where(first, a[...], b[...]) for a, b in zip(pairs[::2], pairs[1::2])]
+    keys = refs[7 : 7 + n_shift]
+    keep_ref, give_ref = refs[7 + n_shift : 9 + n_shift]
+    back_refs = refs[9 + n_shift :]
     live = got()
     keep, give = split_queries(*queries)
+    key = [k[...] for k in keys]
     down = [(dots(keep, k), dots(give, k)) for k in key]
     ahead = [d[0].T for d in down]
     for k in range(n_shift):
@@ -223,10 +222,8 @@
         (z, y, x, c) for z in range(deep) for y in range(2) for x in range(wide) for c in range(2)
     ]
 
-    def moved(value, to, reverse=False, cores=(0, 1)):
-        perm = [
-            (flat(*p), flat(*to(*p))) for p in places if p[3] in cores and to(*p) is not None
-        ]
+    def moved(value, to, reverse=False):
+        perm = [(flat(*p), flat(*to(*p))) for p in places if to(*p) is not None]
         return lax.ppermute(value, AXES, [(b, a) for a, b in perm] if reverse else perm)
 
     def swap(z, y, x, c):
@@ -273,9 +270,7 @@
     twin = moved(unit, swap)
     corner_rows = moved(unit, corner)
     (pair,) = call(join_kernel, [unit, twin], [((2 * rows, width), bf16)])
-    keys = []
-    for j in range(n_shift):
-        keys += [moved(pair, shift(j), cores=(c,)) for c in range(2)]
+    keys = [moved(pair, shift(j)) for j in range(n_shift)]
     direct = moved(pair, side)
     corner_twin = moved(corner_rows, swap)
     relayed = moved(direct, swap)

time: 42.6 us -> 43.1 us (1.012)
  waiting for transfers between devices: 19.7 us -> 20.3 us
    ppermute x13 -> x12, waiting for transfers between devices: 19.7 us -> 20.3 us  [moved(): lax.ppermute(value, AXES, [(b, a) for a, b in perm] if reverse else perm)]
    ppermute x13 -> x12, starting transfers between devices: 17.9 us -> 17.9 us  [moved(): lax.ppermute(value, AXES, [(b, a) for a, b in perm] if reverse else perm)]
  transfers between devices with their start and end apart: 13 -> 12, of which waited for: 6 -> 6; matrix products, arithmetic and copies ran while one was open for 0% -> 0% of each run, Pallas kernels for 2% -> 2%
where the time goes in v1:
time: 43.1 us; the launch traced here: 42.9 us
  waiting for transfers between devices  20.3 us (47%)
  starting transfers between devices  17.9 us (42%)
  Pallas kernels  3.12 us (7%)
  local copies, waits for them, and re-layouts  0.92 us (2%)
  between operations  0.72 us (2%)
    ppermute x12, waiting for transfers between devices, moved(): lax.ppermute(value, AXES, [(b, a) for a, b in perm] if reverse else perm)  20.3 us
    ppermute x12, starting transfers between devices, moved(): lax.ppermute(value, AXES, [(b, a) for a, b in perm] if reverse else perm)  17.9 us
    pallas_call x7, Pallas kernels, call(): pl.pallas_call(kernel, out_shape=[(pltpu.VMEM if keep else jax.ShapeDtype...  3.12 us
    unnamed x2, local copies, waits for them, and re-layouts  0.92 us
  transfers between devices with their start and end apart: 12, of which 6 were waited for; matrix products, arithmetic and copies ran while one was open for 0% of the time, Pallas kernels for 2%

profile of v1, /device:TPU:0, one launch (start us, length us, event | category | flops | bytes accessed | tf_op | source)
XLA Modules:
  0.0 42.9 jit_solution(8213138182798294418)
XLA Ops:
  0.6 0.0 copy-start
  0.6 0.9 %copy-done = bf16[96,1024]{1,0:T(8,128)(2,1)S(1)} copy-done((bf16[96,1024]{1,0:T(8,128)(2,1)S(1)}, bf16[96,1024]{1,0:T(8,128)(2,1)}, u32[]{:S(2)}) %copy-start) | copy-done | bytes 196632
  1.6 0.1 shard_map.30.a_ref
  1.7 0.6 %collective-permute-start = (bf16[96,1024]{1,0:T(8,128)(2,1)S(1)}, bf16[96,1024]{1,0:T(8,128)(2,1)S(1)}, u32[]{:S(2)}, u32[]{:S(2)}) collective-permute-start(bf16[96,1024]{1,0:T(8,128)(2,1)S(1)} %shard_map.30.a_ref), channel_id=1, source_target_pairs={{0,1},{1,0},{2,3},{3,2},{4,5},{5,4},{6,7},{7,6},{8,9},{9,8},{10,11... | collective-permute-start | bytes 589832 | tf_op jit(solution)/shard_map/ppermute | solution.py:227
  2.3 1.1 %collective-permute-done.b_ref = bf16[96,1024]{1,0:T(8,128)(2,1)S(1)} collective-permute-done((bf16[96,1024]{1,0:T(8,128)(2,1)S(1)}, bf16[96,1024]{1,0:T(8,128)(2,1)S(1)}, u32[]{:S(2)}, u32[]{:S(2)}) %collective-permute-start) | collective-permute-done | bytes 196640 | tf_op jit(solution)/shard_map/ppermute | solution.py:227
  3.4 2.9 %collective-permute-start.1 = (bf16[192,1024]{1,0:T(8,128)(2,1)S(1)}, bf16[192,1024]{1,0:T(8,128)(2,1)S(1)}, u32[]{:S(2)}, u32[]{:S(2)}) collective-permute-start(bf16[192,1024]{1,0:T(8,128)(2,1)S(1)} %shard_map.31.pair.refs_0_), channel_id=1, source_target_pairs={{0,2},{1,5},{2,0},{3,7},{4,6},{5,1},{6,4},{7,3},{8,10},{9,13},{10,... | collective-permute-start | bytes 1179656 | tf_op jit(solution)/shard_map/ppermute | solution.py:227
  6.3 1.5 %collective-permute-start.3 = (bf16[96,1024]{1,0:T(8,128)(2,1)S(1)}, bf16[96,1024]{1,0:T(8,128)(2,1)S(1)}, u32[]{:S(2)}, u32[]{:S(2)}) collective-permute-start(bf16[96,1024]{1,0:T(8,128)(2,1)S(1)} %shard_map.30.a_ref), channel_id=1, source_target_pairs={{0,6},{1,7},{2,4},{3,5},{4,2},{5,3},{6,0},{7,1},{8,14},{9,15},{10,... | collective-permute-start | bytes 589832 | tf_op jit(solution)/shard_map/ppermute | solution.py:227
  7.8 6.4 %collective-permute-done.1.refs_0_.refs_1_ = bf16[192,1024]{1,0:T(8,128)(2,1)S(1)} collective-permute-done((bf16[192,1024]{1,0:T(8,128)(2,1)S(1)}, bf16[192,1024]{1,0:T(8,128)(2,1)S(1)}, u32[]{:S(2)}, u32[]{:S(2)}) %collective-permute-start.1) | collective-permute-done | bytes 393248 | tf_op jit(solution)/shard_map/ppermute | solution.py:227
  14.1 0.0 collective-permute-start.2
  14.1 5.0 %collective-permute-start.5 = (bf16[192,1024]{1,0:T(8,128)(2,1)S(1)}, bf16[192,1024]{1,0:T(8,128)(2,1)S(1)}, u32[]{:S(2)}, u32[]{:S(2)}) collective-permute-start(bf16[192,1024]{1,0:T(8,128)(2,1)S(1)} %shard_map.31.pair.refs_0_), channel_id=1, source_target_pairs={{0,16},{1,9},{2,18},{3,11},{4,20},{5,13},{6,22},{7,15},{9,17},{11,... | collective-permute-start | bytes 1179656 | tf_op jit(solution)/shard_map/ppermute | solution.py:227
  19.2 0.0 collective-permute-done.3.refs_1_.refs_3_
  19.2 0.1 collective-permute-start.4
  19.3 0.4 shard_map.32.refs_5_
  19.7 1.0 %collective-permute-done.4.refs_1_.refs_4_ = bf16[96,1024]{1,0:T(8,128)(2,1)S(1)} collective-permute-done((bf16[96,1024]{1,0:T(8,128)(2,1)S(1)}, bf16[96,1024]{1,0:T(8,128)(2,1)S(1)}, u32[]{:S(2)}, u32[]{:S(2)}) %collective-permute-start.4) | collective-permute-done | bytes 196640 | tf_op jit(solution)/shard_map/ppermute | solution.py:227
  20.7 0.0 collective-permute-done.2.refs_0_.refs_2_
  20.7 0.4 shard_map.33.refs_6_
  21.1 6.1 %collective-permute-done.5.refs_7_ = bf16[192,1024]{1,0:T(8,128)(2,1)S(1)} collective-permute-done((bf16[192,1024]{1,0:T(8,128)(2,1)S(1)}, bf16[192,1024]{1,0:T(8,128)(2,1)S(1)}, u32[]{:S(2)}, u32[]{:S(2)}) %collective-permute-start.5) | collective-permute-done | bytes 393248 | tf_op jit(solution)/shard_map/ppermute | solution.py:227
  27.2 1.3 %shard_map.34 = (f32[16,384]{1,0:T(8,128)S(1)}, f32[16,384]{1,0:T(8,128)S(1)}, f32[16,192]{1,0:T(8,128)S(1)}) custom-call(bf16[192,1024]{1,0:T(8,128)(2,1)S(1)} %shard_map.31.pair.refs_0_, bf16[192,1024]{1,0:T(8,128)(2,1)S(1)} %collective-permute-done.1.refs_0_.refs_1_, bf16[192,1024]{1,0:T(8,128)(2,1)S(1)} %collective-permute-done.2.refs_0_.refs_2_, ...), custom_call_target="tpu_custom_call" | custom-call | tf_op jit(solution)/shard_map/pallas_call | solution.py:202
  28.5 2.1 %collective-permute-start.6 = (f32[16,384]{1,0:T(8,128)S(1)}, f32[16,384]{1,0:T(8,128)S(1)}, u32[]{:S(2)}, u32[]{:S(2)}) collective-permute-start(f32[16,384]{1,0:T(8,128)S(1)} %get-tuple-element.11), channel_id=1, source_target_pairs={{0,1},{1,0},{2,3},{3,2},{4,5},{5,4},{6,7},{7,6},{8,9},{9,8},{10,11... | collective-permute-start | bytes 73736 | tf_op jit(solution)/shard_map/ppermute | solution.py:227
  30.6 1.3 %collective-permute-start.10 = (f32[16,192]{1,0:T(8,128)S(1)}, f32[16,192]{1,0:T(8,128)S(1)}, u32[]{:S(2)}, u32[]{:S(2)}) collective-permute-start(f32[16,192]{1,0:T(8,128)S(1)} %get-tuple-element.15), channel_id=1, source_target_pairs={{16,0},{9,1},{18,2},{11,3},{20,4},{13,5},{22,6},{15,7},{17,9},{19,... | collective-permute-start | bytes 36872 | tf_op jit(solution)/shard_map/ppermute | solution.py:227
  31.9 0.0 collective-permute-done.6.got_ref
  31.9 0.1 shard_map.35
  32.0 1.5 %collective-permute-start.8 = (f32[16,192]{1,0:T(8,128)S(1)}, f32[16,192]{1,0:T(8,128)S(1)}, u32[]{:S(2)}, u32[]{:S(2)}) collective-permute-start(f32[16,192]{1,0:T(8,128)S(1)} %get-tuple-element.14), channel_id=1, source_target_pairs={{2,0},{5,1},{0,2},{7,3},{6,4},{1,5},{4,6},{3,7},{10,8},{13,9},{8,1... | collective-permute-start | bytes 36872 | tf_op jit(solution)/shard_map/ppermute | solution.py:227
  33.5 3.6 %collective-permute-done.10.refs_0_ = f32[16,192]{1,0:T(8,128)S(1)} collective-permute-done((f32[16,192]{1,0:T(8,128)S(1)}, f32[16,192]{1,0:T(8,128)S(1)}, u32[]{:S(2)}, u32[]{:S(2)}) %collective-permute-start.10) | collective-permute-done | bytes 12320 | tf_op jit(solution)/shard_map/ppermute | solution.py:227
  37.2 0.0 collective-permute-start.11
  37.2 0.0 collective-permute-done.8.direct
  37.2 0.5 %collective-permute-start.9 = (f32[16,192]{1,0:T(8,128)S(1)}, f32[16,192]{1,0:T(8,128)S(1)}, u32[]{:S(2)}, u32[]{:S(2)}) collective-permute-start(f32[16,192]{1,0:T(8,128)S(1)} %collective-permute-done.8.direct), channel_id=1, source_target_pairs={{0,1},{1,0},{2,3},{3,2},{4,5},{5,4},{6,7},{7,6},{8,9},{9,8},{10,11... | collective-permute-start | bytes 36872 | tf_op jit(solution)/shard_map/ppermute | solution.py:227
  37.7 2.5 %collective-permute-start.7 = (f32[16,96]{1,0:T(8,128)S(1)}, f32[16,96]{1,0:T(8,128)S(1)}, u32[]{:S(2)}, u32[]{:S(2)}) collective-permute-start(f32[16,96]{1,0:T(8,128)S(1)} %get-tuple-element.13), channel_id=1, source_target_pairs={{6,0},{7,1},{4,2},{5,3},{2,4},{3,5},{0,6},{1,7},{14,8},{15,9},{12,... | collective-permute-start | bytes 18440 | tf_op jit(solution)/shard_map/ppermute | solution.py:227
  40.1 0.0 collective-permute-done.11.refs_1_
  40.1 2.1 %collective-permute-done.7.corner = f32[16,96]{1,0:T(8,128)S(1)} collective-permute-done((f32[16,96]{1,0:T(8,128)S(1)}, f32[16,96]{1,0:T(8,128)S(1)}, u32[]{:S(2)}, u32[]{:S(2)}) %collective-permute-start.7) | collective-permute-done | bytes 6176 | tf_op jit(solution)/shard_map/ppermute | solution.py:227
  42.2 0.0 collective-permute-done.9.relayed
  42.2 0.7 %shard_map.36 = (f32[8,96]{1,0:T(8,128)}, f32[1,96]{1,0:T(1,128)}) custom-call(f32[16,96]{1,0:T(8,128)S(1)} %get-tuple-element.12.own, f32[16,96]{1,0:T(8,128)S(1)} %collective-permute-done.7.corner, f32[16,192]{1,0:T(8,128)S(1)} %collective-permute-done.8.direct, f32[16,192]{1,0:T(8,128)S(1)} %collective-permute-done.9.relayed, ...), custom_call_target="tpu_custom_call" | custom-call | tf_op jit(solution)/shard_map/pallas_call | solution.py:202
  (1 shorter events, 0.0 us)
Async XLA Ops:
  0.6 0.9 %copy-start = (bf16[96,1024]{1,0:T(8,128)(2,1)S(1)}, bf16[96,1024]{1,0:T(8,128)(2,1)}, u32[]{:S(2)}) copy-start(bf16[96,1024]{1,0:T(8,128)(2,1)} %x_ref.1) | copy-start | bytes 589828
  1.7 1.6 %collective-permute-start = (bf16[96,1024]{1,0:T(8,128)(2,1)S(1)}, bf16[96,1024]{1,0:T(8,128)(2,1)S(1)}, u32[]{:S(2)}, u32[]{:S(2)}) collective-permute-start(bf16[96,1024]{1,0:T(8,128)(2,1)S(1)} %shard_map.30.a_ref), channel_id=1, source_target_pairs={{0,1},{1,0},{2,3},{3,2},{4,5},{5,4},{6,7},{7,6},{8,9},{9,8},{10,11... | collective-permute-start | bytes 589832 | tf_op jit(solution)/shard_map/ppermute | solution.py:227
  3.4 10.8 %collective-permute-start.1 = (bf16[192,1024]{1,0:T(8,128)(2,1)S(1)}, bf16[192,1024]{1,0:T(8,128)(2,1)S(1)}, u32[]{:S(2)}, u32[]{:S(2)}) collective-permute-start(bf16[192,1024]{1,0:T(8,128)(2,1)S(1)} %shard_map.31.pair.refs_0_), channel_id=1, source_target_pairs={{0,2},{1,5},{2,0},{3,7},{4,6},{5,1},{6,4},{7,3},{8,10},{9,13},{10,... | collective-permute-start | bytes 1179656 | tf_op jit(solution)/shard_map/ppermute | solution.py:227
  6.3 12.9 %collective-permute-start.3 = (bf16[96,1024]{1,0:T(8,128)(2,1)S(1)}, bf16[96,1024]{1,0:T(8,128)(2,1)S(1)}, u32[]{:S(2)}, u32[]{:S(2)}) collective-permute-start(bf16[96,1024]{1,0:T(8,128)(2,1)S(1)} %shard_map.30.a_ref), channel_id=1, source_target_pairs={{0,6},{1,7},{2,4},{3,5},{4,2},{5,3},{6,0},{7,1},{8,14},{9,15},{10,... | collective-permute-start | bytes 589832 | tf_op jit(solution)/shard_map/ppermute | solution.py:227
  14.1 6.6 %collective-permute-start.2 = (bf16[192,1024]{1,0:T(8,128)(2,1)S(1)}, bf16[192,1024]{1,0:T(8,128)(2,1)S(1)}, u32[]{:S(2)}, u32[]{:S(2)}) collective-permute-start(bf16[192,1024]{1,0:T(8,128)(2,1)S(1)} %collective-permute-done.1.refs_0_.refs_1_), channel_id=1, source_target_pairs={{0,1},{1,0},{2,3},{3,2},{4,5},{5,4},{6,7},{7,6},{8,9},{9,8},{10,11... | collective-permute-start | bytes 1179656 | tf_op jit(solution)/shard_map/ppermute | solution.py:227
  14.1 13.1 %collective-permute-start.5 = (bf16[192,1024]{1,0:T(8,128)(2,1)S(1)}, bf16[192,1024]{1,0:T(8,128)(2,1)S(1)}, u32[]{:S(2)}, u32[]{:S(2)}) collective-permute-start(bf16[192,1024]{1,0:T(8,128)(2,1)S(1)} %shard_map.31.pair.refs_0_), channel_id=1, source_target_pairs={{0,16},{1,9},{2,18},{3,11},{4,20},{5,13},{6,22},{7,15},{9,17},{11,... | collective-permute-start | bytes 1179656 | tf_op jit(solution)/shard_map/ppermute | solution.py:227
  19.2 1.5 %collective-permute-start.4 = (bf16[96,1024]{1,0:T(8,128)(2,1)S(1)}, bf16[96,1024]{1,0:T(8,128)(2,1)S(1)}, u32[]{:S(2)}, u32[]{:S(2)}) collective-permute-start(bf16[96,1024]{1,0:T(8,128)(2,1)S(1)} %collective-permute-done.3.refs_1_.refs_3_), channel_id=1, source_target_pairs={{0,1},{1,0},{2,3},{3,2},{4,5},{5,4},{6,7},{7,6},{8,9},{9,8},{10,11... | collective-permute-start | bytes 589832 | tf_op jit(solution)/shard_map/ppermute | solution.py:227
  28.5 3.4 %collective-permute-start.6 = (f32[16,384]{1,0:T(8,128)S(1)}, f32[16,384]{1,0:T(8,128)S(1)}, u32[]{:S(2)}, u32[]{:S(2)}) collective-permute-start(f32[16,384]{1,0:T(8,128)S(1)} %get-tuple-element.11), channel_id=1, source_target_pairs={{0,1},{1,0},{2,3},{3,2},{4,5},{5,4},{6,7},{7,6},{8,9},{9,8},{10,11... | collective-permute-start | bytes 73736 | tf_op jit(solution)/shard_map/ppermute | solution.py:227
  30.6 6.5 %collective-permute-start.10 = (f32[16,192]{1,0:T(8,128)S(1)}, f32[16,192]{1,0:T(8,128)S(1)}, u32[]{:S(2)}, u32[]{:S(2)}) collective-permute-start(f32[16,192]{1,0:T(8,128)S(1)} %get-tuple-element.15), channel_id=1, source_target_pairs={{16,0},{9,1},{18,2},{11,3},{20,4},{13,5},{22,6},{15,7},{17,9},{19,... | collective-permute-start | bytes 36872 | tf_op jit(solution)/shard_map/ppermute | solution.py:227
  32.0 5.1 %collective-permute-start.8 = (f32[16,192]{1,0:T(8,128)S(1)}, f32[16,192]{1,0:T(8,128)S(1)}, u32[]{:S(2)}, u32[]{:S(2)}) collective-permute-start(f32[16,192]{1,0:T(8,128)S(1)} %get-tuple-element.14), channel_id=1, source_target_pairs={{2,0},{5,1},{0,2},{7,3},{6,4},{1,5},{4,6},{3,7},{10,8},{13,9},{8,1... | collective-permute-start | bytes 36872 | tf_op jit(solution)/shard_map/ppermute | solution.py:227
  37.2 3.0 %collective-permute-start.11 = (f32[16,192]{1,0:T(8,128)S(1)}, f32[16,192]{1,0:T(8,128)S(1)}, u32[]{:S(2)}, u32[]{:S(2)}) collective-permute-start(f32[16,192]{1,0:T(8,128)S(1)} %collective-permute-done.10.refs_0_), channel_id=1, source_target_pairs={{0,1},{1,0},{2,3},{3,2},{4,5},{5,4},{6,7},{7,6},{8,9},{9,8},{10,11... | collective-permute-start | bytes 36872 | tf_op jit(solution)/shard_map/ppermute | solution.py:227
  37.2 5.1 %collective-permute-start.9 = (f32[16,192]{1,0:T(8,128)S(1)}, f32[16,192]{1,0:T(8,128)S(1)}, u32[]{:S(2)}, u32[]{:S(2)}) collective-permute-start(f32[16,192]{1,0:T(8,128)S(1)} %collective-permute-done.8.direct), channel_id=1, source_target_pairs={{0,1},{1,0},{2,3},{3,2},{4,5},{5,4},{6,7},{7,6},{8,9},{9,8},{10,11... | collective-permute-start | bytes 36872 | tf_op jit(solution)/shard_map/ppermute | solution.py:227
  37.7 4.5 %collective-permute-start.7 = (f32[16,96]{1,0:T(8,128)S(1)}, f32[16,96]{1,0:T(8,128)S(1)}, u32[]{:S(2)}, u32[]{:S(2)}) collective-permute-start(f32[16,96]{1,0:T(8,128)S(1)} %get-tuple-element.13), channel_id=1, source_target_pairs={{6,0},{7,1},{4,2},{5,3},{2,4},{3,5},{0,6},{1,7},{14,8},{15,9},{12,... | collective-permute-start | bytes 18440 | tf_op jit(solution)/shard_map/ppermute | solution.py:227
